TPU v7x, 512 devices: a whole 4x8x8 slice. The times are simulated.
512 devices in a mesh: seq: 32 (over z_hi, y, core), mp: 16 (over z_lo, x).
Axes of the slice: x: 4, y: 8, z: 8 (z_hi: 2, z_lo: 4; z = z_hi * 4 + z_lo), core: 2. Of those that a mesh axis runs over, the one named last changes fastest.
Arguments:
- inputs: bfloat16 [32768, 4096], P('seq', 'mp'), may hold values from -6 to 6
- conv_weight: bfloat16 [4, 4096], P(None, 'mp'), may hold values from -3 to 3
- conv_bias: bfloat16 [4096], P('mp'), may hold values from -3 to 3
- doc_start: int32 [32768], P('seq'), may hold values from 0 to 32767, as said below
- counts: int32 [32], P('seq'), may hold values from 341 to 1024
Outputs:
- gram: float32 [4096, 4096], P('seq', 'mp')
Inputs may be any that keep to these rules, and one draw needn't show every extreme that they name: doc_start is never above the token's own position, and for t > 0 either doc_start[t] == t or doc_start[t] == doc_start[t - 1]; doc_start[0] is 0.
All inputs are finite; a program needn't handle non-finite values.
Results may differ from a plain program's by a relative error of at most 0.0003.
Values may be sent and summed in bfloat16 or wider, within the bound.
No kernel may reach another device: no remote copies, remote signals or barrier semaphores. Data moves between devices by JAX's collectives and lax.ppermute only.
A program may use at most 64 MiB of HBM per device.

v0:
```python
import jax
import jax.numpy as jnp
from jax import lax
from jax.sharding import Mesh
from jax.sharding import PartitionSpec as P

SEQ = ("seq_0", "seq_1", "seq_2")


def sent_to_all(x, axis):
    copies = jnp.broadcast_to(x, (lax.axis_size(axis), *x.shape))
    return lax.all_to_all(copies, axis, split_axis=0, concat_axis=0, tiled=True)


def taken_together(x, axis):
    everything = sent_to_all(x, axis)
    return jnp.sum(everything, axis=0)


def passed_along(x, axis, by):
    peers = lax.axis_size(axis)
    pairs = [(i, i + by) for i in range(peers) if 0 <= i + by < peers]
    return lax.ppermute(x, axis, pairs)


def cut_along(x, dim, peers):
    dims = x.shape
    pieces = x.reshape(*dims[:dim], peers, dims[dim] // peers, *dims[dim + 1 :])
    return jnp.moveaxis(pieces, dim, 0)


def summed_on_arrival(x, axis, dim):
    pieces = cut_along(x, dim, lax.axis_size(axis))
    arrived = lax.all_to_all(pieces, axis, split_axis=0, concat_axis=0, tiled=True)
    return arrived.sum(axis=0)


def sum_in_two_steps(x, axes, dim):
    far, near = axes
    pieces = cut_along(x, dim, lax.axis_size(far))
    nearer = summed_on_arrival(pieces, near, dim + 1)
    arrived = lax.all_to_all(nearer, far, split_axis=0, concat_axis=0, tiled=True)
    return arrived.sum(axis=0)


def causal_conv(extended, weights, bias, position, doc_start, length):
    kernel_len = weights.shape[0]
    summed = jnp.zeros((length, weights.shape[1]), jnp.float32) + bias.astype(jnp.float32)
    for lag in range(kernel_len):
        window = extended[kernel_len - 1 - lag : kernel_len - 1 - lag + length].astype(jnp.float32)
        usable = position - lag >= doc_start
        summed = summed + jnp.where(usable[:, None], weights[lag].astype(jnp.float32) * window, 0.0)
    return jax.nn.silu(summed).astype(jnp.bfloat16)


def on_device(inputs, conv_weight, conv_bias, doc_start, counts):
    row_count = inputs.shape[0]
    kernel_len = conv_weight.shape[0]
    position = lax.axis_index(SEQ) * row_count + jnp.arange(row_count, dtype=jnp.int32)
    counted = jnp.arange(row_count, dtype=jnp.int32) < counts[0]
    token_total = taken_together(counts.astype(jnp.float32)[0], SEQ)
    prior = passed_along(inputs[row_count - (kernel_len - 1) :], SEQ, 1)
    extended = jnp.concatenate([prior, inputs], axis=0)
    own_feats = causal_conv(extended, conv_weight, conv_bias, position, doc_start, row_count)
    kept = jnp.where(counted[:, None], own_feats, jnp.zeros_like(own_feats))
    whole = lax.all_gather(own_feats, "mp", axis=1, tiled=True)
    summed = sum_in_two_steps(
        lax.dot_general(whole, kept, (((0,), (0,)), ((), ())), preferred_element_type=jnp.float32),
        (("seq_0", "seq_1"), "seq_2"),
        0,
    )
    return summed / token_total


def solution(mesh):
    torus = Mesh(mesh.devices.reshape(2, 8, 2, mesh.shape["mp"]), ("seq_0", "seq_1", "seq_2", "mp"))
    placed = (P(SEQ, "mp"), P(None, "mp"), P("mp"), P(SEQ), P(SEQ))
    return jax.shard_map(
        on_device, mesh=torus, in_specs=placed, out_specs=P(SEQ, "mp"), check_vma=False
    )
```

profile of v0, /device:TPU:33, one launch (start us, length us, event | category | flops | bytes accessed | tf_op | source)
XLA Modules:
  0.0 267.8 jit_solution(6630288082526933012)
XLA Ops:
  6.5 0.0 all-gather.2.cloned.1.call-start
  6.5 0.7 slice.26
  7.2 2.9 %collective-permute-start = (bf16[3,256]{1,0:T(4,128)(2,1)S(1)}, bf16[3,256]{1,0:T(4,128)(2,1)S(1)}, u32[]{:S(2)}, u32[]{:S(2)}) collective-permute-start(bf16[3,256]{1,0:T(4,128)(2,1)S(1)} %slice.26), channel_id=1, source_target_pairs={{0,16},{16,32},{32,48},{48,64},{64,80},{80,96},{96,112},{112,128},... | collective-permute-start | bytes 4616 | tf_op jit(solution)/shard_map/ppermute | solution.py:23
  10.1 0.7 fusion.6
  10.8 0.8 slice_convert_fusion.3
  11.6 0.7 convert_element_type.29
  12.3 0.0 collective-permute-done
  12.3 4.5 %multiply_convert_fusion = bf16[1024,256]{1,0:T(8,128)(2,1)} fusion(bf16[1024,256]{1,0:T(8,128)(2,1)} %param.5, bf16[3,256]{1,0:T(4,128)(2,1)S(1)} %collective-permute-done, f32[256]{0:T(256)S(1)} %bitcast.16, f32[256]{0:T(256)S(1)} %bitcast.17, f32[256]{0:T(256)S(1)} %bitcast.15, f32[256]{0:T(256)S(1)} %bitcast.14, f32[256]{0:T(256)S(1)} %convert_element_type.29, ...), kind=kLoop, calls=%fused_computation.1 | loop fusion | flops 7864320 | bytes 1059328 | tf_op jit(solution)/shard_map/convert_element_type | solution.py:53
  16.8 0.0 all-gather.2.cloned.1.call-update
  17.5 121.6 %all-gather.2.cloned.1.call-done = bf16[1024,4096]{1,0:T(8,128)(2,1)} async-done(((bf16[1024,256]{1,0:T(8,128)(2,1)}), bf16[1024,4096]{1,0:T(8,128)(2,1)}) %all-gather.2.cloned.1.call-update) | async-done | bytes 8388624 | tf_op jit(solution)/shard_map/all_gather | solution.py:66
  139.0 6.0 %fusion.2 = f32[4096,256]{1,0:T(8,128)S(1)} fusion(bf16[1024,4096]{1,0:T(8,128)(2,1)} %all-gather.2.cloned.1.call-done, bf16[1024,256]{1,0:T(8,128)(2,1)} %multiply_convert_fusion, pred[1024]{0:T(1024)(128)(4,1)S(1)} %iota_compare_fusion), kind=kOutput, calls=%fused_computation.7 | convolution fusion | flops 2147745792 | bytes 13108224 | tf_op jit(solution)/shard_map/dot_general | solution.py:68
  145.0 0.4 copy.12
  145.5 17.4 %all_to_all.16 = f32[2,16,128,256]{3,2,1,0:T(8,128)} all-to-all(f32[2,16,128,256]{3,2,1,0:T(8,128)S(1)} %bitcast.12), channel_id=1, replica_groups=mesh['seq_0'=2,'seq_1'=8,'seq_2'=2,'mp'=16] {'seq_2'}, dimensions={0} | all-to-all | bytes 8388608 | tf_op jit(solution)/shard_map/all_to_all | solution.py:34
  162.9 0.6 broadcast_in_dim.61
  163.5 11.9 %all-to-all-start.2 = ((f32[32,1,1]{2,1,0:T(1,128)}), f32[32,1,1]{2,1,0:T(1,128)S(1)}, u32[]{:S(2)}, u32[]{:S(2)}) async-start(f32[32,1,1]{2,1,0:T(1,128)} %broadcast_in_dim.61), calls=%async_computation.2 | async-start | bytes 32768 | tf_op jit(solution)/shard_map/all_to_all | solution.py:12
  175.4 4.0 %reduce_sum.27 = f32[16,128,256]{2,1,0:T(8,128)} reduce(f32[2,16,128,256]{3,2,1,0:T(8,128)} %all_to_all.16, f32[]{:T(128)} %constant.32.clone.1), dimensions={0}, to_apply=%region_0.0 | reduce | flops 524288 | bytes 6291460 | tf_op jit(solution)/shard_map/reduce_sum | solution.py:35
  179.5 2.8 %all-to-all-done.2 = f32[32,1,1]{2,1,0:T(1,128)S(1)} async-done(((f32[32,1,1]{2,1,0:T(1,128)}), f32[32,1,1]{2,1,0:T(1,128)S(1)}, u32[]{:S(2)}, u32[]{:S(2)}) %all-to-all-start.2) | async-done | bytes 160 | tf_op jit(solution)/shard_map/all_to_all | solution.py:12
  182.2 8.7 %all-to-all-start.1 = ((f32[16,128,256]{2,1,0:T(8,128)}), f32[16,128,256]{2,1,0:T(8,128)S(1)}, u32[]{:S(2)}, u32[]{:S(2)}) async-start(f32[16,128,256]{2,1,0:T(8,128)} %reduce_sum.27), calls=%async_computation.1 | async-start | bytes 4194304 | tf_op jit(solution)/shard_map/all_to_all | solution.py:42
  191.0 0.7 reduce_sum.29
  191.6 67.9 %all-to-all-done.1 = f32[16,128,256]{2,1,0:T(8,128)S(1)} async-done(((f32[16,128,256]{2,1,0:T(8,128)}), f32[16,128,256]{2,1,0:T(8,128)S(1)}, u32[]{:S(2)}, u32[]{:S(2)}) %all-to-all-start.1) | async-done | bytes 2097184 | tf_op jit(solution)/shard_map/all_to_all | solution.py:42
  259.6 0.1 reduce_sum.28
  259.7 1.3 broadcast_divide_fusion
  (1 shorter events, 0.0 us)
Async XLA Ops:
  6.5 132.5 %all-gather.2.cloned.1.call-start = ((), (), s32[]{:S(2)}) async-start(), calls=%async_computation.3 | async-start | bytes 8912896 | tf_op jit(solution)/shard_map/all_gather | solution.py:66
  7.2 5.1 %collective-permute-start = (bf16[3,256]{1,0:T(4,128)(2,1)S(1)}, bf16[3,256]{1,0:T(4,128)(2,1)S(1)}, u32[]{:S(2)}, u32[]{:S(2)}) collective-permute-start(bf16[3,256]{1,0:T(4,128)(2,1)S(1)} %slice.26), channel_id=1, source_target_pairs={{0,16},{16,32},{32,48},{48,64},{64,80},{80,96},{96,112},{112,128},... | collective-permute-start | bytes 4616 | tf_op jit(solution)/shard_map/ppermute | solution.py:23
  163.5 18.7 %all-to-all-start.2 = ((f32[32,1,1]{2,1,0:T(1,128)}), f32[32,1,1]{2,1,0:T(1,128)S(1)}, u32[]{:S(2)}, u32[]{:S(2)}) async-start(f32[32,1,1]{2,1,0:T(1,128)} %broadcast_in_dim.61), calls=%async_computation.2 | async-start | bytes 32768 | tf_op jit(solution)/shard_map/all_to_all | solution.py:12
  182.2 77.3 %all-to-all-start.1 = ((f32[16,128,256]{2,1,0:T(8,128)}), f32[16,128,256]{2,1,0:T(8,128)S(1)}, u32[]{:S(2)}, u32[]{:S(2)}) async-start(f32[16,128,256]{2,1,0:T(8,128)} %reduce_sum.27), calls=%async_computation.1 | async-start | bytes 4194304 | tf_op jit(solution)/shard_map/all_to_all | solution.py:42
Sparse Core Ops, SparseCore 0:
  16.9 122.0 all-gather.1
where the time goes:
time: 268 us
  waiting for transfers between devices  192 us (72%)
  starting transfers between devices  23.5 us (9%)
  blocking collectives  17.4 us (6%)
  between operations  14.1 us (5%)
  other arithmetic  12.8 us (5%)
  matrix products  5.99 us (2%)
    all_gather x1, waiting for transfers between devices, on_device(): whole = lax.all_gather(own_feats, 'mp', axis=1, tiled=True)  122 us
    all_to_all x1, waiting for transfers between devices, sum_in_two_steps(): lax.all_to_all(nearer, far, split_axis=0, concat_axis=0, tiled=True)  67.9 us
    all_to_all x1, blocking collectives, summed_on_arrival(): lax.all_to_all(pieces, axis, split_axis=0, concat_axis=0, tiled=True)  17.4 us
    all_to_all x1, starting transfers between devices, sent_to_all(): return lax.all_to_all(copies, axis, split_axis=0, concat_axis=0, tiled=True)  11.9 us
    all_to_all x1, starting transfers between devices, sum_in_two_steps(): lax.all_to_all(nearer, far, split_axis=0, concat_axis=0, tiled=True)  8.74 us
    dot_general x1, matrix products, on_device(): lax.dot_general(whole, kept, (((0,), (0,)), ((), ())), preferred_element_...  5.99 us
  transfers between devices with their start and end apart: 4, of which 3 were waited for; matrix products, arithmetic and copies ran while one was open for 3% of the time, Pallas kernels for 0%

commit v1 on v0

--- a/solution.py
+++ b/solution.py
@@ -63,7 +63,9 @@
     extended = jnp.concatenate([prior, inputs], axis=0)
     own_feats = causal_conv(extended, conv_weight, conv_bias, position, doc_start, row_count)
     kept = jnp.where(counted[:, None], own_feats, jnp.zeros_like(own_feats))
-    whole = lax.all_gather(own_feats, "mp", axis=1, tiled=True)
+    whole = jnp.concatenate(
+        lax.all_to_all(jnp.stack([own_feats] * lax.axis_size("mp")), "mp", 0, 0), axis=1
+    )
     summed = sum_in_two_steps(
         lax.dot_general(whole, kept, (((0,), (0,)), ((), ())), preferred_element_type=jnp.float32),
         (("seq_0", "seq_1"), "seq_2"),

time: 268 us -> 313 us (1.17)
  the two profiles are of different devices: /device:TPU:33 before, /device:TPU:92 now
where the time goes in v1:
time: 313 us
  waiting for transfers between devices  248 us (79%)
  starting transfers between devices  30.8 us (10%)
  other arithmetic  12.2 us (4%)
  blocking collectives  8.32 us (3%)
  local copies, waits for them, and re-layouts  6.24 us (2%)
  matrix products  5.84 us (2%)
    all_to_all x1, waiting for transfers between devices, on_device(): lax.all_to_all(jnp.stack([own_feats] * lax.axis_size('mp')), 'mp', 0, 0)  183 us
    all_to_all x1, waiting for transfers between devices, sum_in_two_steps(): lax.all_to_all(nearer, far, split_axis=0, concat_axis=0, tiled=True)  60 us
    all_to_all x1, starting transfers between devices, sent_to_all(): return lax.all_to_all(copies, axis, split_axis=0, concat_axis=0, tiled=True)  12.7 us
    all_to_all x1, starting transfers between devices, on_device(): lax.all_to_all(jnp.stack([own_feats] * lax.axis_size('mp')), 'mp', 0, 0)  9.34 us
    all_to_all x1, blocking collectives, summed_on_arrival(): lax.all_to_all(pieces, axis, split_axis=0, concat_axis=0, tiled=True)  8.32 us
    all_to_all x1, starting transfers between devices, sum_in_two_steps(): lax.all_to_all(nearer, far, split_axis=0, concat_axis=0, tiled=True)  6.9 us
  transfers between devices with their start and end apart: 4, of which 4 were waited for; matrix products, arithmetic and copies ran while one was open for 2% of the time, Pallas kernels for 0%

profile of v1, /device:TPU:92, one launch (start us, length us, event | category | flops | bytes accessed | tf_op | source)
XLA Modules:
  0.0 312.6 jit_solution(6863636739102600136)
XLA Ops:
  0.0 0.7 slice.26
  0.7 1.9 collective-permute-start
  2.6 0.7 fusion.6
  3.3 0.8 slice_convert_fusion.3
  4.2 0.7 convert_element_type.29
  4.8 0.8 collective-permute-done
  5.6 3.9 %multiply_convert_fusion = bf16[1024,256]{1,0:T(8,128)(2,1)S(1)} fusion(bf16[1024,256]{1,0:T(8,128)(2,1)} %param.5, bf16[3,256]{1,0:T(4,128)(2,1)S(1)} %collective-permute-done, f32[256]{0:T(256)S(1)} %bitcast.24, f32[256]{0:T(256)S(1)} %bitcast.25, f32[256]{0:T(256)S(1)} %bitcast.23, f32[256]{0:T(256)S(1)} %bitcast.22, f32[256]{0:T(256)S(1)} %convert_element_type.29, ...), kind=kLoop, calls=%fused_computation.1 | loop fusion | flops 7864320 | bytes 1059328 | tf_op jit(solution)/shard_map/convert_element_type | solution.py:53
  9.5 0.2 copy.11
  9.7 4.3 %stack.2 = bf16[16,1024,256]{1,2,0:T(8,128)(2,1)} broadcast(bf16[1024,256]{0,1:T(8,128)(2,1)S(1)} %copy.11), dimensions={1,2} | broadcast | bytes 8912896 | tf_op jit(solution)/shard_map/stack | solution.py:67
  14.0 9.3 %all-to-all-start = ((bf16[16,1024,256]{1,2,0:T(8,128)(2,1)}), bf16[16,1024,256]{1,2,0:T(8,128)(2,1)}, u32[]{:S(2)}, u32[]{:S(2)}) async-start(bf16[16,1024,256]{1,2,0:T(8,128)(2,1)} %stack.2), calls=%async_computation | async-start | bytes 16777216 | tf_op jit(solution)/shard_map/all_to_all | solution.py:67
  24.0 182.5 %all-to-all-done = bf16[16,1024,256]{1,2,0:T(8,128)(2,1)} async-done(((bf16[16,1024,256]{1,2,0:T(8,128)(2,1)}), bf16[16,1024,256]{1,2,0:T(8,128)(2,1)}, u32[]{:S(2)}, u32[]{:S(2)}) %all-to-all-start) | async-done | bytes 8388640 | tf_op jit(solution)/shard_map/all_to_all | solution.py:67
  206.5 5.8 %convolution_bitcast_fusion = f32[2,16,128,256]{3,2,0,1:T(8,128)S(1)} fusion(bf16[16,2,128,1024]{3,2,1,0:T(8,128)(2,1)} %bitcast.7, bf16[1024,256]{1,0:T(8,128)(2,1)S(1)} %multiply_convert_fusion, pred[1024]{0:T(1024)(128)(4,1)S(1)} %iota_compare_fusion), kind=kOutput, calls=%fused_computation | convolution fusion | flops 2147745792 | bytes 13108224 | tf_op jit(solution)/shard_map/dot_general | solution.py:70
  212.4 0.4 copy.12
  212.8 8.3 %all_to_all.21 = f32[2,16,128,256]{3,2,1,0:T(8,128)} all-to-all(f32[2,16,128,256]{3,2,1,0:T(8,128)S(1)} %copy.12), channel_id=1, replica_groups=mesh['seq_0'=2,'seq_1'=8,'seq_2'=2,'mp'=16] {'seq_2'}, dimensions={0} | all-to-all | bytes 8388608 | tf_op jit(solution)/shard_map/all_to_all | solution.py:34
  221.1 0.6 broadcast_in_dim.61
  221.8 12.7 %all-to-all-start.3 = ((f32[32,1,1]{2,1,0:T(1,128)}), f32[32,1,1]{2,1,0:T(1,128)S(1)}, u32[]{:S(2)}, u32[]{:S(2)}) async-start(f32[32,1,1]{2,1,0:T(1,128)} %broadcast_in_dim.61), calls=%async_computation.3 | async-start | bytes 32768 | tf_op jit(solution)/shard_map/all_to_all | solution.py:12
  234.4 4.1 %reduce_sum.27 = f32[16,128,256]{2,1,0:T(8,128)} reduce(f32[2,16,128,256]{3,2,1,0:T(8,128)} %all_to_all.21, f32[]{:T(128)} %constant.32.clone.1), dimensions={0}, to_apply=%region_0.0 | reduce | flops 524288 | bytes 6291460 | tf_op jit(solution)/shard_map/reduce_sum | solution.py:35
  238.5 5.2 %all-to-all-done.3 = f32[32,1,1]{2,1,0:T(1,128)S(1)} async-done(((f32[32,1,1]{2,1,0:T(1,128)}), f32[32,1,1]{2,1,0:T(1,128)S(1)}, u32[]{:S(2)}, u32[]{:S(2)}) %all-to-all-start.3) | async-done | bytes 160 | tf_op jit(solution)/shard_map/all_to_all | solution.py:12
  243.7 6.9 %all-to-all-start.2 = ((f32[16,128,256]{2,1,0:T(8,128)}), f32[16,128,256]{2,1,0:T(8,128)S(1)}, u32[]{:S(2)}, u32[]{:S(2)}) async-start(f32[16,128,256]{2,1,0:T(8,128)} %reduce_sum.27), calls=%async_computation.2 | async-start | bytes 4194304 | tf_op jit(solution)/shard_map/all_to_all | solution.py:42
  250.6 0.6 reduce_sum.29
  251.2 60.0 %all-to-all-done.2 = f32[16,128,256]{2,1,0:T(8,128)S(1)} async-done(((f32[16,128,256]{2,1,0:T(8,128)}), f32[16,128,256]{2,1,0:T(8,128)S(1)}, u32[]{:S(2)}, u32[]{:S(2)}) %all-to-all-start.2) | async-done | bytes 2097184 | tf_op jit(solution)/shard_map/all_to_all | solution.py:42
  311.2 0.1 reduce_sum.28
  311.4 1.2 broadcast_divide_fusion
  (1 shorter events, 0.0 us)
Async XLA Ops:
  0.7 4.9 %collective-permute-start = (bf16[3,256]{1,0:T(4,128)(2,1)S(1)}, bf16[3,256]{1,0:T(4,128)(2,1)S(1)}, u32[]{:S(2)}, u32[]{:S(2)}) collective-permute-start(bf16[3,256]{1,0:T(4,128)(2,1)S(1)} %slice.26), channel_id=1, source_target_pairs={{0,16},{16,32},{32,48},{48,64},{64,80},{80,96},{96,112},{112,128},... | collective-permute-start | bytes 4616 | tf_op jit(solution)/shard_map/ppermute | solution.py:23
  14.0 192.5 %all-to-all-start = ((bf16[16,1024,256]{1,2,0:T(8,128)(2,1)}), bf16[16,1024,256]{1,2,0:T(8,128)(2,1)}, u32[]{:S(2)}, u32[]{:S(2)}) async-start(bf16[16,1024,256]{1,2,0:T(8,128)(2,1)} %stack.2), calls=%async_computation | async-start | bytes 16777216 | tf_op jit(solution)/shard_map/all_to_all | solution.py:67
  221.8 21.9 %all-to-all-start.3 = ((f32[32,1,1]{2,1,0:T(1,128)}), f32[32,1,1]{2,1,0:T(1,128)S(1)}, u32[]{:S(2)}, u32[]{:S(2)}) async-start(f32[32,1,1]{2,1,0:T(1,128)} %broadcast_in_dim.61), calls=%async_computation.3 | async-start | bytes 32768 | tf_op jit(solution)/shard_map/all_to_all | solution.py:12
  243.7 67.6 %all-to-all-start.2 = ((f32[16,128,256]{2,1,0:T(8,128)}), f32[16,128,256]{2,1,0:T(8,128)S(1)}, u32[]{:S(2)}, u32[]{:S(2)}) async-start(f32[16,128,256]{2,1,0:T(8,128)} %reduce_sum.27), calls=%async_computation.2 | async-start | bytes 4194304 | tf_op jit(solution)/shard_map/all_to_all | solution.py:42
